TPU v7x, 16 devices: a 4x2x1 block of a 4x4x8 slice. The times are simulated.
16 devices in a mesh: dp: 2 (over y, z), tp: 8 (over x, core).
Axes of the slice: x: 4, y: 2, z: 1, core: 2. Of those that a mesh axis runs over, the one named last changes fastest.
The devices are a block of a 4x4x8 slice.
Arguments:
- x: bfloat16 [4096, 5120], P('dp'), parts along dimension 0
- w_gate: bfloat16 [5120, 27648], P(None, 'tp')
- w_up: bfloat16 [5120, 27648], P(None, 'tp')
- w_down: bfloat16 [27648, 5120], P('tp')
Outputs:
- output: bfloat16 [4096, 5120], P('dp'), parts along dimension 0
There are 2 independent parts. A program takes and returns all parts, laid end to end along the dimension named above; an argument that names none is the same for every part.
All inputs are finite; a program needn't handle non-finite values.
Results may differ from a plain program's by a relative error of at most 0.016.
Values are sent between devices in bfloat16 or wider.
A program may use at most 768 MiB of HBM per device.

v0:
```python
import jax
import jax.numpy as jnp
from jax import lax
from jax.sharding import PartitionSpec as P


def solution(mesh):
    def step(x, w_gate, w_up, w_down):
        gate = jnp.dot(x, w_gate, preferred_element_type=jnp.float32)
        up = jnp.dot(x, w_up, preferred_element_type=jnp.float32)
        hidden = (jax.nn.silu(gate) * up).astype(jnp.bfloat16)
        term = jnp.dot(hidden, w_down, preferred_element_type=jnp.float32).astype(jnp.bfloat16)
        return lax.psum(term, "tp")

    return jax.shard_map(
        step,
        mesh=mesh,
        in_specs=(P("dp", None), P(None, "tp"), P(None, "tp"), P("tp", None)),
        out_specs=P("dp", None),
        check_vma=False,
    )
```

profile of v0, /device:TPU:113, one launch (start us, length us, event | category | flops | bytes accessed | tf_op | source)
XLA Modules:
  0.0 513.2 jit_solution(15582260837217316810)
XLA Ops:
  6.5 0.0 all-reduce.2.cloned.1.call-start
  6.6 87.9 %fusion = f32[2048,3456]{1,0:T(8,128)} fusion(bf16[2048,5120]{1,0:T(8,128)(2,1)} %param.4, bf16[5120,3456]{1,0:T(8,128)(2,1)} %param.5), kind=kOutput, calls=%fused_computation.2 | convolution fusion | flops 72477573120 | bytes 84672512 | tf_op jit(solution)/shard_map/dot_general | solution.py:9
  94.4 93.6 %multiply_convert_fusion = bf16[2048,3456]{1,0:T(8,128)(2,1)} fusion(f32[2048,3456]{1,0:T(8,128)} %fusion, bf16[2048,5120]{1,0:T(8,128)(2,1)} %param.4, bf16[5120,3456]{1,0:T(8,128)(2,1)} %param.6), kind=kOutput, calls=%fused_computation | convolution fusion | flops 72520040448 | bytes 98828288 | tf_op jit(solution)/shard_map/dot_general | solution.py:10
  188.0 84.2 %convolution_convert_fusion = bf16[2048,5120]{1,0:T(8,128)(2,1)} fusion(bf16[2048,3456]{1,0:T(8,128)(2,1)} %multiply_convert_fusion, bf16[3456,5120]{1,0:T(8,128)(2,1)} %param.7), kind=kOutput, calls=%fused_computation.1 | convolution fusion | flops 72488058880 | bytes 70516736 | tf_op jit(solution)/shard_map/dot_general | solution.py:12
  272.2 0.1 all-reduce.2.cloned.1.call-update
  272.3 216.7 %all-reduce.2.cloned.1.call-done = bf16[2048,5120]{1,0:T(8,128)(2,1)} async-done(((bf16[2048,5120]{1,0:T(8,128)(2,1)}), bf16[2048,5120]{1,0:T(8,128)(2,1)}) %all-reduce.2.cloned.1.call-update) | async-done | bytes 20971536 | tf_op jit(solution)/shard_map/psum | solution.py:13
  489.0 17.3 %copy.6 = bf16[2048,5120]{1,0:T(8,128)(2,1)} copy(bf16[2048,5120]{1,0:T(8,128)(2,1)} %all-reduce.2.cloned.1.call-done) | data formatting | bytes 41943040
Async XLA Ops:
  6.5 482.5 %all-reduce.2.cloned.1.call-start = ((), (), s32[]{:S(2)}) async-start(), calls=%async_computation | async-start | bytes 41943040 | tf_op jit(solution)/shard_map/psum | solution.py:13
Sparse Core Ops, SparseCore 0:
  272.4 216.5 all-reduce.1
where the time goes:
time: 514 us; the launch traced here: 513 us
  matrix products  266 us (52%)
  waiting for transfers between devices  217 us (42%)
  local copies, waits for them, and re-layouts  17.3 us (3%)
  between operations  13.4 us (3%)
    psum x1, waiting for transfers between devices, step(): return lax.psum(term, 'tp')  217 us
    dot_general x1, matrix products, step(): up = jnp.dot(x, w_up, preferred_element_type=jnp.float32)  93.6 us
    dot_general x1, matrix products, step(): gate = jnp.dot(x, w_gate, preferred_element_type=jnp.float32)  87.9 us
    dot_general x1, matrix products, step(): jnp.dot(hidden, w_down, preferred_element_type=jnp.float32)  84.2 us
    unnamed x1, local copies, waits for them, and re-layouts  17.3 us
  transfers between devices with their start and end apart: 1, of which 1 were waited for; matrix products, arithmetic and copies ran while one was open for 0% of the time, Pallas kernels for 0%

commit v1 on v0

v1 whole, which is shorter than its diff:
```python
import functools

import jax
import jax.numpy as jnp
from jax import lax
from jax.experimental import pallas as pl
from jax.experimental.pallas import tpu as pltpu
from jax.sharding import PartitionSpec as P

BF16, F32 = jnp.bfloat16, jnp.float32
MESH = pl.DeviceIdType.MESH
CORES = 2
ROWS = 512
GU_COLS = 384
D_COLS = 512


def block(n, x, w_gate, w_up, w_down):
    rows, d = x.shape
    f = w_gate.shape[1]
    chips = n // CORES
    assert chips == 4
    half = d // CORES
    r_, gb, db = ROWS, GU_COLS, D_COLS
    nr, ng, nd = rows // r_, f // gb, half // db
    assert nr * r_ == rows and ng * gb == f and nd * db == half
    assert ng == 9 and nd == 5
    piece = r_ // chips
    hp = piece // 2

    def kernel(x_ref, wg_ref, wu_ref, wd_ref, y_ref, wdp_ref, xb, wgu, wdb, hid, sb, rly, dirb, relb,
               x_sem, g_sem, d_sem, wd_send, wd_recv, h_send, h_recv, credit,
               rly_send, rly_recv, dir_send, dir_recv, rel_send, rel_recv,
               ag_send, ag_recv, agp_send, fw_send, fw_recv, loc_sem, p_send, p_recv):
        me = lax.axis_index("tp")
        chip, core = me // CORES, lax.rem(me, CORES)
        right_chip, left_chip = lax.rem(chip + 1, chips), lax.rem(chip + chips - 1, chips)
        far_chip = lax.rem(chip + 2, chips)
        right, left = right_chip * CORES + core, left_chip * CORES + core
        partner = chip * CORES + (1 - core)
        sides = (right, left)
        my_half = core * half
        partner_half = (1 - core) * half

        def ds(start, size, m):
            return pl.ds(pl.multiple_of(start, m), size)

        def remote(src, dst, send, recv, to):
            return pltpu.make_async_remote_copy(
                src_ref=src, dst_ref=dst, send_sem=send, recv_sem=recv,
                device_id={"tp": to}, device_id_type=MESH)

        def x_copy(r):
            return pltpu.make_async_copy(x_ref.at[ds(r * r_, r_, r_)], xb, x_sem)

        def gu_copies(j, slot):
            cols = ds(j * gb, gb, 128)
            return (pltpu.make_async_copy(wg_ref.at[:, cols], wgu.at[slot, :, pl.ds(0, gb)], g_sem.at[slot, 0]),
                    pltpu.make_async_copy(wu_ref.at[:, cols], wgu.at[slot, :, pl.ds(gb, gb)], g_sem.at[slot, 1]))

        def d_copies(k, slot):
            return (pltpu.make_async_copy(wd_ref.at[:, ds(my_half + k * db, db, 128)], wdb.at[slot, pl.ds(0, f)], d_sem.at[slot, 0]),
                    pltpu.make_async_copy(wdp_ref.at[:, ds(k * db, db, 128)], wdb.at[slot, pl.ds(f, f)], d_sem.at[slot, 1]))

        def wd_copy(k):
            return remote(wd_ref.at[:, ds(partner_half + k * db, db, 128)], wdp_ref.at[:, ds(k * db, db, 128)],
                          wd_send.at[k], wd_recv.at[k], partner)

        def h_copy(j):
            return remote(hid.at[:, ds(j * gb, gb, 128)], hid.at[:, ds(f + j * gb, gb, 128)], h_send, h_recv, partner)

        def h_all():
            return remote(hid.at[:, pl.ds(0, f)], hid.at[:, pl.ds(f, f)], h_send, h_recv, partner)

        def rows_of(q, part):
            return ds(q * piece + part * hp, hp, hp)

        def rly_copy(k, s):
            return remote(sb.at[k, rows_of(far_chip, s)], rly.at[s, k], rly_send.at[s, k], rly_recv.at[s, k], sides[s])

        def dir_copy(k, s):
            to_chip = (right_chip, left_chip)[s]
            return remote(sb.at[k, rows_of(to_chip, 1 - s)], dirb.at[s, k], dir_send.at[s, k], dir_recv.at[s, k], sides[s])

        def rel_copy(k, s):
            to_chip = (right_chip, left_chip)[s]
            return remote(sb.at[k, rows_of(to_chip, s)], relb.at[s, k], rel_send.at[s, k], rel_recv.at[s, k], sides[s])

        def y_at(r, q, k, part=None):
            cols = ds(my_half + k * db, db, 128)
            if part is None:
                return y_ref.at[ds(r * r_ + q * piece, piece, piece), cols]
            return y_ref.at[ds(r * r_ + q * piece + part * hp, hp, hp), cols]

        def own_piece(k):
            return sb.at[k, ds(chip * piece, piece, piece)]

        def loc_copy(r, k):
            return pltpu.make_async_copy(own_piece(k), y_at(r, chip, k), loc_sem.at[k])

        def ag_copy(r, k, s):
            return remote(own_piece(k), y_at(r, chip, k), ag_send.at[s, k], ag_recv.at[s, k], sides[s])

        def agp_copy(r, k):
            return remote(own_piece(k), y_at(r, chip, k), agp_send.at[k], p_recv, partner)

        def fw_copy(r, k, s):
            q = (left_chip, right_chip)[s]
            return remote(y_at(r, q, k, s), y_at(r, q, k, s), fw_send.at[s, k], fw_recv.at[s, k], sides[s])

        def p_copy(r, k, q):
            return remote(y_at(r, q, k), y_at(r, q, k), p_send, p_recv, partner)

        def first_sends(k):
            for s in range(2):
                rly_copy(k, s).start()
            for s in range(2):
                dir_copy(k, s).start()

        def stage1(k):
            for s in range(2):
                rly_copy(k, s).wait_recv()
                rr = rows_of((right_chip, left_chip)[s], s)
                sb[k, rr] = (sb[k, rr].astype(F32) + rly[s, k].astype(F32)).astype(BF16)
            for s in range(2):
                rel_copy(k, s).start()

        def stage2(r, k):
            for s in range(2):
                rly_copy(k, s).wait_send()
                dir_copy(k, s).wait()
                rel_copy(k, s).wait_recv()
            for part in range(2):
                rr = rows_of(chip, part)
                from_left = (relb if part == 0 else dirb)[0, k].astype(F32)
                from_right = (relb if part == 1 else dirb)[1, k].astype(F32)
                sb[k, rr] = (sb[k, rr].astype(F32) + from_left + from_right).astype(BF16)
            for s in range(2):
                ag_copy(r, k, s).start()
            agp_copy(r, k).start()
            loc_copy(r, k).start()

        def stage3(r, k):
            for s in range(2):
                rel_copy(k, s).wait_send()
                ag_copy(r, k, s).wait_recv()
            for s in range(2):
                fw_copy(r, k, s).start()
            p_copy(r, k, left_chip).start()
            p_copy(r, k, right_chip).start()
            loc_copy(r, k).wait()

        def stage4(r, k):
            for s in range(2):
                ag_copy(r, k, s).wait_send()
                fw_copy(r, k, s).wait()
            agp_copy(r, k).wait_send()
            p_copy(r, k, far_chip).start()

        def events(j, r):
            @pl.when(j < 2)
            def _():
                stage1(j + 3)

            @pl.when(j < 4)
            def _():
                stage2(r, j + 1)

            @pl.when(jnp.logical_and(j >= 2, j < 7))
            def _():
                stage3(r, j - 2)

            @pl.when(j >= 4)
            def _():
                stage4(r, j - 4)

        x_copy(0).start()
        for j in range(2):
            for c in gu_copies(j, j):
                c.start()
        barrier = pltpu.get_barrier_semaphore()
        for to in (right, left, partner):
            pl.semaphore_signal(barrier, inc=1, device_id={"tp": to}, device_id_type=MESH)
        pl.semaphore_wait(barrier, 3)
        for k in range(nd):
            wd_copy(k).start()

        def start_down(r, k):
            @pl.when(r == 0)
            def _():
                wd_copy(k).wait_recv()
            for c in d_copies(k, lax.rem(k, 2)):
                c.start()

        def chunk(r, _):
            x_copy(r).wait()

            def gate_up(j, _):
                slot = lax.rem(r * ng + j, 2)
                for c in gu_copies(j, slot):
                    c.wait()

                @pl.when(r > 0)
                def _():
                    events(j, r - 1)
                acc = jnp.dot(xb[...], wgu[slot], preferred_element_type=F32)
                gate, up = acc[:, :gb], acc[:, gb:]
                hid[:, ds(j * gb, gb, 128)] = (jax.nn.silu(gate) * up).astype(BF16)

                @pl.when(jnp.logical_and(r > 0, j == 0))
                def _():
                    pl.semaphore_wait(credit, 1)

                @pl.when(jnp.logical_or(r < nr - 1, j < ng - 2))
                def _():
                    for c in gu_copies(lax.rem(j + 2, ng), slot):
                        c.start()
                h_copy(j).start()

                @pl.when(j == 3)
                def _():
                    start_down(r, 0)

                @pl.when(j == 5)
                def _():
                    start_down(r, 1)
                return 0

            lax.fori_loop(0, ng, gate_up, 0)

            @pl.when(r < nr - 1)
            def _():
                x_copy(r + 1).start()
            h_all().wait()

            def down(k, _):
                slot = lax.rem(k, 2)
                for c in d_copies(k, slot):
                    c.wait()
                acc = jnp.dot(hid[...], wdb[slot], preferred_element_type=F32)
                sb[k] = acc.astype(BF16)

                @pl.when(k < nd - 2)
                def _():
                    start_down(r, k + 2)
                first_sends(k)

                @pl.when(k >= 2)
                def _():
                    stage1(k - 2)

                @pl.when(k == nd - 1)
                def _():
                    stage2(r, 0)
                return 0

            lax.fori_loop(0, nd, down, 0)

            @pl.when(r < nr - 1)
            def _():
                pl.semaphore_signal(credit, inc=1, device_id={"tp": partner}, device_id_type=MESH)
            return 0

        lax.fori_loop(0, nr, chunk, 0)

        def tail(j, _):
            events(j, nr - 1)
            return 0

        lax.fori_loop(0, ng, tail, 0)
        for k in range(nd):
            wd_copy(k).wait_send()
        sent = y_ref.at[pl.ds(0, rows - rows // chips), ds(my_half, half, 128)]
        came = y_ref.at[:, ds(partner_half, half, 128)]
        remote(sent, sent, p_send, p_recv, partner).wait_send()
        remote(came, came, p_send, p_recv, partner).wait_recv()

    dma = pltpu.SemaphoreType.DMA
    y, _ = pl.pallas_call(
        kernel,
        out_shape=(jax.ShapeDtypeStruct((rows, d), BF16), jax.ShapeDtypeStruct((f, half), BF16)),
        in_specs=[pl.BlockSpec(memory_space=pl.ANY)] * 4,
        out_specs=(pl.BlockSpec(memory_space=pl.ANY),) * 2,
        scratch_shapes=[
            pltpu.VMEM((r_, d), BF16),
            pltpu.VMEM((2, d, 2 * gb), BF16),
            pltpu.VMEM((2, CORES * f, db), BF16),
            pltpu.VMEM((r_, CORES * f), BF16),
            pltpu.VMEM((nd, r_, db), BF16),
            pltpu.VMEM((2, nd, hp, db), BF16),
            pltpu.VMEM((2, nd, hp, db), BF16),
            pltpu.VMEM((2, nd, hp, db), BF16),
            dma, dma((2, 2)), dma((2, 2)),
            dma((nd,)), dma((nd,)), dma, dma, pltpu.SemaphoreType.REGULAR,
            dma((2, nd)), dma((2, nd)), dma((2, nd)), dma((2, nd)), dma((2, nd)), dma((2, nd)),
            dma((2, nd)), dma((2, nd)), dma((nd,)), dma((2, nd)), dma((2, nd)), dma((nd,)), dma, dma,
        ],
        compiler_params=pltpu.CompilerParams(
            collective_id=0, has_side_effects=True, vmem_limit_bytes=67043328),
        cost_estimate=pl.CostEstimate(flops=6 * rows * d * f, bytes_accessed=2 * 3 * d * f * nr, transcendentals=rows * f),
        name="mlp_block",
    )(x, w_gate, w_up, w_down)
    return y


def solution(mesh):
    return jax.shard_map(
        functools.partial(block, mesh.shape["tp"]),
        mesh=mesh,
        in_specs=(P("dp", None), P(None, "tp"), P(None, "tp"), P("tp", None)),
        out_specs=P("dp", None),
        check_vma=False,
    )
```

time: 514 us -> 317 us (0.62)
  Pallas kernels: 0 us -> 299 us
  matrix products: 266 us -> 0 us
  waiting for transfers between devices: 217 us -> 0 us
  between operations: 13.4 us -> 0.01 us
    pallas_call x0 -> x1, Pallas kernels: none -> 299 us  [block(): pl.pallas_call(kernel, out_shape=(jax.ShapeDtypeStruct((rows, d), BF16),...]
    dot_general x3 -> x0, matrix products: 266 us -> none  [the longest x1 93.6 us: step(): up = jnp.dot(x, w_up, preferred_element_type=jnp.float32)]
    psum x1 -> x0, waiting for transfers between devices: 217 us -> none  [step(): return lax.psum(term, 'tp')]
  transfers between devices with their start and end apart: 1 -> 0, of which waited for: 1 -> 0; matrix products, arithmetic and copies ran while one was open for 0% -> 0% of each run, Pallas kernels for 0% -> 0%
where the time goes in v1:
time: 317 us
  Pallas kernels  299 us (94%)
  local copies, waits for them, and re-layouts  17.3 us (5%)
    pallas_call x1, Pallas kernels, block(): pl.pallas_call(kernel, out_shape=(jax.ShapeDtypeStruct((rows, d), BF16),...  299 us
    unnamed x1, local copies, waits for them, and re-layouts  17.3 us

profile of v1, /device:TPU:113, one launch (start us, length us, event | category | flops | bytes accessed | tf_op | source)
XLA Modules:
  0.0 316.7 jit_solution(343729767174999772)
XLA Ops:
  0.0 299.4 %mlp_block.1 = (bf16[2048,5120]{1,0:T(8,128)(2,1)}, bf16[3456,2560]{1,0:T(8,128)(2,1)}) custom-call(bf16[2048,5120]{1,0:T(8,128)(2,1)} %x_ref.1, bf16[5120,3456]{1,0:T(8,128)(2,1)} %wg_ref.1, bf16[5120,3456]{1,0:T(8,128)(2,1)} %wu_ref.1, bf16[3456,5120]{1,0:T(8,128)(2,1)} %wd_ref.1), custom_call_target="tpu_custom_call" | custom-call | flops 217432719360 | bytes 424673280 | tf_op jit(solution)/shard_map/mlp_block/pallas_call | solution.py:279
  299.4 17.3 %copy.6 = bf16[2048,5120]{1,0:T(8,128)(2,1)} copy(bf16[2048,5120]{1,0:T(8,128)(2,1)} %get-tuple-element.6) | data formatting | bytes 41943040

commit v2 on v1

v2 whole, which is shorter than its diff:
```python
import functools

import jax
import jax.numpy as jnp
from jax import lax
from jax.experimental import pallas as pl
from jax.experimental.pallas import tpu as pltpu
from jax.sharding import PartitionSpec as P

BF16, F32 = jnp.bfloat16, jnp.float32
MESH = pl.DeviceIdType.MESH
CORES = 2
CHUNKS = (4, 4, 4, 4)
KERNEL_VMEM = 42_500_000
GU_COLS = 384
D_COLS = 512


def join(d, *parts):
    sizes = [p.shape[0] for p in parts]
    starts = [sum(sizes[:i]) for i in range(len(parts))]

    def kernel(*refs):
        *ins, y_ref, sem = refs
        copies = [
            pltpu.make_async_copy(ref.at[:, pl.ds(0, d)], y_ref.at[pl.ds(start, n)], sem.at[i])
            for i, (ref, start, n) in enumerate(zip(ins, starts, sizes))
        ]
        for c in copies:
            c.start()
        for c in copies:
            c.wait()

    return pl.pallas_call(
        kernel,
        out_shape=jax.ShapeDtypeStruct((sum(sizes), d), BF16),
        in_specs=[pl.BlockSpec(memory_space=pltpu.VMEM)] * len(parts),
        out_specs=pl.BlockSpec(memory_space=pl.ANY),
        scratch_shapes=[pltpu.SemaphoreType.DMA((len(parts),))],
        compiler_params=pltpu.CompilerParams(vmem_limit_bytes=4_000_000),
        name="join",
    )(*parts)


def block(n, x, w_gate, w_up, w_down):
    rows, d = x.shape
    f = w_gate.shape[1]
    chips = n // CORES
    assert chips == 4
    half = d // CORES
    gb, db = GU_COLS, D_COLS
    nr, ng, nd = len(CHUNKS), f // gb, half // db
    unit = rows // sum(CHUNKS)
    size = [c * unit for c in CHUNKS]
    base = [sum(size[:r]) for r in range(nr)]
    top = max(size)
    assert sum(size) == rows and ng * gb == f and nd * db == half
    assert ng == 9 and nd == 5
    parts = 2 * chips
    assert all(c % (16 * parts) == 0 for c in size)
    assert size[0] == size[-1] == top

    def kernel(x_ref, wg_ref, wu_ref, wd_ref, hid, mid_ref, xb, early_ref, wdp_ref, wgu, wdb, sb, rly, dirb, relb,
               x_sem, g_sem, d_sem, wd_send, wd_recv, h_send, h_recv, credit,
               rly_send, rly_recv, dir_send, dir_recv, rel_send, rel_recv,
               ag_send, ag_recv, agp_send, fw_send, fw_recv, loc_sem, p_send, p_recv):
        me = lax.axis_index("tp")
        chip, core = me // CORES, lax.rem(me, CORES)
        right_chip, left_chip = lax.rem(chip + 1, chips), lax.rem(chip + chips - 1, chips)
        far_chip = lax.rem(chip + 2, chips)
        right, left = right_chip * CORES + core, left_chip * CORES + core
        partner = chip * CORES + (1 - core)
        sides = (right, left)
        my_half = core * half
        partner_half = (1 - core) * half

        def ds(start, size, m):
            return pl.ds(pl.multiple_of(start, m), size)

        def remote(src, dst, send, recv, to):
            return pltpu.make_async_remote_copy(
                src_ref=src, dst_ref=dst, send_sem=send, recv_sem=recv,
                device_id={"tp": to}, device_id_type=MESH)

        def x_copy(r):
            return pltpu.make_async_copy(x_ref.at[pl.ds(base[r], size[r])], xb.at[pl.ds(0, size[r])], x_sem)

        def gu_copies(j, slot):
            cols = ds(j * gb, gb, 128)
            return (pltpu.make_async_copy(wg_ref.at[:, cols], wgu.at[slot, :, pl.ds(0, gb)], g_sem.at[slot, 0]),
                    pltpu.make_async_copy(wu_ref.at[:, cols], wgu.at[slot, :, pl.ds(gb, gb)], g_sem.at[slot, 1]))

        def d_copies(k, slot):
            return (pltpu.make_async_copy(wd_ref.at[:, ds(my_half + k * db, db, 128)], wdb.at[slot, pl.ds(0, f)], d_sem.at[slot, 0]),
                    pltpu.make_async_copy(wdp_ref.at[:, ds(k * db, db, 128)], wdb.at[slot, pl.ds(f, f)], d_sem.at[slot, 1]))

        def wd_copy(k):
            return remote(wd_ref.at[:, ds(partner_half + k * db, db, 128)], wdp_ref.at[:, ds(k * db, db, 128)],
                          wd_send.at[k], wd_recv.at[k], partner)

        def h_copy(r, j):
            at = pl.ds(0, size[r])
            return remote(hid.at[at, ds(j * gb, gb, 128)], hid.at[at, ds(f + j * gb, gb, 128)], h_send, h_recv, partner)

        def h_all(r):
            at = pl.ds(0, size[r])
            return remote(hid.at[at, pl.ds(0, f)], hid.at[at, pl.ds(f, f)], h_send, h_recv, partner)

        def rows_of(r, q, part):
            hp = size[r] // parts
            return ds(q * 2 * hp + part * hp, hp, hp)

        def rly_copy(r, k, s):
            return remote(sb.at[k, rows_of(r, far_chip, s)], rly.at[s, k, pl.ds(0, size[r] // parts)], rly_send.at[s, k], rly_recv.at[s, k], sides[s])

        def dir_copy(r, k, s):
            to_chip = (right_chip, left_chip)[s]
            return remote(sb.at[k, rows_of(r, to_chip, 1 - s)], dirb.at[s, k, pl.ds(0, size[r] // parts)], dir_send.at[s, k], dir_recv.at[s, k], sides[s])

        def rel_copy(r, k, s):
            to_chip = (right_chip, left_chip)[s]
            return remote(sb.at[k, rows_of(r, to_chip, s)], relb.at[s, k, pl.ds(0, size[r] // parts)], rel_send.at[s, k], rel_recv.at[s, k], sides[s])

        def place(r):
            return (early_ref, 0) if r == 0 else (xb, 0) if r == nr - 1 else (mid_ref, base[r] - base[1])

        def group(r):
            return 0 if r == 0 else 2 if r == nr - 1 else 1

        def y_at(r, q, k, part=None):
            cols = ds(my_half + k * db, db, 128)
            hp = size[r] // parts
            ref, start = place(r)
            if part is None:
                return ref.at[ds(start + q * 2 * hp, 2 * hp, hp), cols]
            return ref.at[ds(start + q * 2 * hp + part * hp, hp, hp), cols]

        def own_piece(r, k):
            hp = size[r] // parts
            return sb.at[k, ds(chip * 2 * hp, 2 * hp, 2 * hp)]

        def loc_copy(r, k):
            return pltpu.make_async_copy(own_piece(r, k), y_at(r, chip, k), loc_sem.at[k])

        def ag_copy(r, k, s):
            return remote(own_piece(r, k), y_at(r, chip, k), ag_send.at[s, k], ag_recv.at[s, k], sides[s])

        def agp_copy(r, k):
            return remote(own_piece(r, k), y_at(r, chip, k), agp_send.at[k], p_recv.at[group(r)], partner)

        def fw_copy(r, k, s):
            q = (left_chip, right_chip)[s]
            return remote(y_at(r, q, k, s), y_at(r, q, k, s), fw_send.at[s, k], fw_recv.at[s, k], sides[s])

        def p_copy(r, k, q):
            return remote(y_at(r, q, k), y_at(r, q, k), p_send.at[group(r)], p_recv.at[group(r)], partner)

        def first_sends(r, k):
            for s in range(2):
                rly_copy(r, k, s).start()
            for s in range(2):
                dir_copy(r, k, s).start()

        def stage1(r, k):
            for s in range(2):
                rly_copy(r, k, s).wait_recv()
                rr = rows_of(r, (right_chip, left_chip)[s], s)
                sb[k, rr] = (sb[k, rr].astype(F32) + rly[s, k, pl.ds(0, size[r] // parts)].astype(F32)).astype(BF16)
            for s in range(2):
                rel_copy(r, k, s).start()

        def stage2(r, k):
            for s in range(2):
                rly_copy(r, k, s).wait_send()
                dir_copy(r, k, s).wait()
                rel_copy(r, k, s).wait_recv()
            at = pl.ds(0, size[r] // parts)
            for part in range(2):
                rr = rows_of(r, chip, part)
                from_left = (relb if part == 0 else dirb)[0, k, at].astype(F32)
                from_right = (relb if part == 1 else dirb)[1, k, at].astype(F32)
                sb[k, rr] = (sb[k, rr].astype(F32) + from_left + from_right).astype(BF16)
            for s in range(2):
                ag_copy(r, k, s).start()
            agp_copy(r, k).start()
            loc_copy(r, k).start()

        def stage3(r, k):
            for s in range(2):
                rel_copy(r, k, s).wait_send()
                ag_copy(r, k, s).wait_recv()
            for s in range(2):
                fw_copy(r, k, s).start()
            p_copy(r, k, left_chip).start()
            p_copy(r, k, right_chip).start()
            loc_copy(r, k).wait()

        def stage4(r, k):
            for s in range(2):
                ag_copy(r, k, s).wait_send()
                fw_copy(r, k, s).wait()
            agp_copy(r, k).wait_send()
            p_copy(r, k, far_chip).start()

        def events(j, r):
            @pl.when(j < 2)
            def _():
                stage1(r, j + 3)

            @pl.when(jnp.logical_and(j >= 1, j < 5))
            def _():
                stage2(r, j)

            @pl.when(jnp.logical_and(j >= 2, j < 7))
            def _():
                stage3(r, j - 2)

            @pl.when(j >= 5)
            def _():
                stage4(r, j - 5)

            @pl.when(j == 8)
            def _():
                stage4(r, 4)

        x_copy(0).start()
        for c in gu_copies(0, 0):
            c.start()
        barrier = pltpu.get_barrier_semaphore()
        for to in (right, left, partner):
            pl.semaphore_signal(barrier, inc=1, device_id={"tp": to}, device_id_type=MESH)
        pl.semaphore_wait(barrier, 3)
        for k in range(nd):
            wd_copy(k).start()

        def start_down(r, k):
            if r == 0:
                wd_copy(k).wait_recv()
            for c in d_copies(k, lax.rem(k, 2)):
                c.start()

        for r in range(nr):
            x_copy(r).wait()
            all_rows = pl.ds(0, size[r])

            def gate_up(j, _):
                slot = lax.rem(r * ng + j, 2)
                for c in gu_copies(j, slot):
                    c.wait()
                if r == 0:
                    @pl.when(j == 0)
                    def _():
                        for c in gu_copies(1, 1):
                            c.start()
                acc = jnp.dot(xb[all_rows], wgu[slot], preferred_element_type=F32)
                gate, up = acc[:, :gb], acc[:, gb:]
                hid[all_rows, ds(j * gb, gb, 128)] = (jax.nn.silu(gate) * up).astype(BF16)

                def refill():
                    for c in gu_copies(lax.rem(j + 2, ng), slot):
                        c.start()
                if r < nr - 1:
                    refill()
                else:
                    pl.when(j < ng - 2)(refill)
                if r > 0:
                    @pl.when(j == 0)
                    def _():
                        pl.semaphore_wait(credit, 1)
                h_copy(r, j).start()

                @pl.when(j == 3)
                def _():
                    start_down(r, 0)

                @pl.when(j == 5)
                def _():
                    start_down(r, 1)
                if r > 0:
                    events(j, r - 1)
                return 0

            lax.fori_loop(0, ng, gate_up, 0)
            if r < nr - 1:
                x_copy(r + 1).start()

            h_all(r).wait()

            def down(k, _):
                slot = lax.rem(k, 2)
                for c in d_copies(k, slot):
                    c.wait()
                acc = jnp.dot(hid[all_rows], wdb[slot], preferred_element_type=F32)
                sb[k, all_rows] = acc.astype(BF16)

                @pl.when(k < nd - 2)
                def _():
                    start_down(r, k + 2)
                first_sends(r, k)

                @pl.when(k >= 2)
                def _():
                    stage1(r, k - 2)

                @pl.when(k == nd - 1)
                def _():
                    stage2(r, 0)
                return 0

            lax.fori_loop(0, nd, down, 0)
            if r < nr - 1:
                pl.semaphore_signal(credit, inc=1, device_id={"tp": partner}, device_id_type=MESH)

        def wait_partner(i, ref):
            n_rows = ref.shape[0]
            sent = ref.at[pl.ds(0, n_rows - n_rows // chips), ds(my_half, half, 128)]
            came = ref.at[:, ds(partner_half, half, 128)]
            remote(sent, sent, p_send.at[i], p_recv.at[i], partner).wait_send()
            remote(came, came, p_send.at[i], p_recv.at[i], partner).wait_recv()

        wait_partner(0, early_ref)
        early_copy = pltpu.make_async_copy(early_ref, hid.at[:, pl.ds(0, d)], x_sem)
        early_copy.start()

        def tail(j, _):
            events(j, nr - 1)
            return 0

        lax.fori_loop(0, ng, tail, 0)
        for k in range(nd):
            wd_copy(k).wait_send()
        wait_partner(1, mid_ref)
        wait_partner(2, xb)
        early_copy.wait()

    dma = pltpu.SemaphoreType.DMA
    first, middle, last, _, _ = pl.pallas_call(
        kernel,
        out_shape=(pltpu.VMEM((top, CORES * f), BF16), pltpu.VMEM((base[-1] - base[1], d), BF16), pltpu.VMEM((top, d), BF16),
                   pltpu.HBM((size[0], d), BF16), pltpu.HBM((f, half), BF16)),
        in_specs=[pl.BlockSpec(memory_space=pl.ANY)] * 4,
        out_specs=tuple(pl.BlockSpec(memory_space=m) for m in (pltpu.VMEM,) * 3 + (pltpu.HBM,) * 2),
        scratch_shapes=[
            pltpu.VMEM((2, d, 2 * gb), BF16),
            pltpu.VMEM((2, CORES * f, db), BF16),
            pltpu.VMEM((nd, top, db), BF16),
            pltpu.VMEM((2, nd, top // parts, db), BF16),
            pltpu.VMEM((2, nd, top // parts, db), BF16),
            pltpu.VMEM((2, nd, top // parts, db), BF16),
            dma, dma((2, 2)), dma((2, 2)),
            dma((nd,)), dma((nd,)), dma, dma, pltpu.SemaphoreType.REGULAR,
            dma((2, nd)), dma((2, nd)), dma((2, nd)), dma((2, nd)), dma((2, nd)), dma((2, nd)),
            dma((2, nd)), dma((2, nd)), dma((nd,)), dma((2, nd)), dma((2, nd)), dma((nd,)), dma((3,)), dma((3,)),
        ],
        compiler_params=pltpu.CompilerParams(
            collective_id=0, has_side_effects=True, vmem_limit_bytes=KERNEL_VMEM),
        cost_estimate=pl.CostEstimate(flops=6 * rows * d * f, bytes_accessed=2 * 3 * d * f * nr, transcendentals=rows * f),
        name="mlp_block",
    )(x, w_gate, w_up, w_down)
    return join(d, first, middle, last)


def solution(mesh):
    return jax.shard_map(
        functools.partial(block, mesh.shape["tp"]),
        mesh=mesh,
        in_specs=(P("dp", None), P(None, "tp"), P(None, "tp"), P("tp", None)),
        out_specs=P("dp", None),
        check_vma=False,
    )
```

time: 317 us -> 291 us (0.918)
  local copies, waits for them, and re-layouts: 17.3 us -> 0 us
  Pallas kernels: 299 us -> 290 us
    unnamed x1 -> x0, local copies, waits for them, and re-layouts: 17.3 us -> none
    pallas_call x1 -> x2, Pallas kernels: 299 us -> 290 us  [the longest x1 283 us: block(): pl.pallas_call(kernel, out_shape=(pltpu.VMEM((top, CORES * f), BF16), plt...]
where the time goes in v2:
time: 291 us
  Pallas kernels  290 us (100%)
    pallas_call x1, Pallas kernels, block(): pl.pallas_call(kernel, out_shape=(pltpu.VMEM((top, CORES * f), BF16), plt...  283 us
    pallas_call x1, Pallas kernels, join(): pl.pallas_call(kernel, out_shape=jax.ShapeDtypeStruct((sum(sizes), d), BF...  7.27 us

profile of v2, /device:TPU:113, one launch (start us, length us, event | category | flops | bytes accessed | tf_op | source)
XLA Modules:
  0.0 290.7 jit_solution(6384733997946910881)
XLA Ops:
  0.0 283.2 %mlp_block.1 = (bf16[512,6912]{1,0:T(8,128)(2,1)S(1)}, bf16[1024,5120]{1,0:T(8,128)(2,1)S(1)}, bf16[512,5120]{1,0:T(8,128)(2,1)S(1)}, bf16[512,5120]{1,0:T(8,128)(2,1)}, bf16[3456,2560]{1,0:T(8,128)(2,1)}) custom-call(bf16[2048,5120]{1,0:T(8,128)(2,1)} %x_ref.1, bf16[5120,3456]{1,0:T(8,128)(2,1)} %wg_ref.1, bf16[5120,3456]{1,0:T(8,128)(2,1)} %wu_ref.1, ...), custom_call_target="tpu_custom_call" | custom-call | flops 217432719360 | bytes 424673280 | tf_op jit(solution)/shard_map/mlp_block/pallas_call | solution.py:337
  283.2 7.3 %join.1 = bf16[2048,5120]{1,0:T(8,128)(2,1)} custom-call(bf16[512,6912]{1,0:T(8,128)(2,1)S(1)} %get-tuple-element.8.refs_0_, bf16[1024,5120]{1,0:T(8,128)(2,1)S(1)} %get-tuple-element.9.refs_1_, bf16[512,5120]{1,0:T(8,128)(2,1)S(1)} %get-tuple-element.10.refs_2_), custom_call_target="tpu_custom_call" | custom-call | tf_op jit(solution)/shard_map/join/pallas_call | solution.py:34
